TPU v7x, 32 devices: a whole 2x2x4 slice. The times are simulated.
32 devices in a mesh: row: 4 (over z), col: 8 (over y, x, core).
Axes of the slice: x: 2, y: 2, z: 4, core: 2. Of those that a mesh axis runs over, the one named last changes fastest.
Arguments:
- eigvecs: bfloat16 [40960, 2048], P('row', 'col'), may hold values from -0.125 to 0.125
- reflectors: bfloat16 [2, 40960, 128], P(None, 'row'), may hold values from -6 to 6
- factors: float32 [2, 128, 128], replicated, may hold values from -0.00024414062 to 0.00024414062
- frequencies: float32 [2048], replicated, may hold values from 0.3 to 3
- region_blocks: int32 [72], P('row'), may hold values from 0 to 319, as said below
Outputs:
- covariance: float32 [9216, 9216], P('row', 'col')
Inputs may be any that keep to these rules, and one draw needn't show every extreme that they name: `region_blocks`: the 72 block numbers are distinct and ascending; exactly 18 of them lie in each consecutive run of 80 block numbers.
All inputs are finite; a program needn't handle non-finite values.
Results may differ from a plain program's by a relative error of at most 0.004.
Values may be sent and summed in bfloat16 or wider, within the bound.
A program may use at most 128 MiB of HBM per device.

v0:
```python
import jax
import jax.numpy as jnp
from jax import lax
from jax.sharding import PartitionSpec as P

BLOCK = 128


def contract_rows(left, right):
    return lax.dot_general(
        left, right, (((0,), (0,)), ((), ())), preferred_element_type=jnp.float32
    )


def contract_cols(left, right):
    return lax.dot_general(
        left, right, (((1,), (1,)), ((), ())), preferred_element_type=jnp.float32
    )


def per_device(eigvecs, reflectors, factors, frequencies, region_blocks):
    highest = lax.Precision.HIGHEST
    first_block = reflectors[0]
    second_block = reflectors[1]
    first_factor = jnp.triu(factors[0])
    second_factor = jnp.triu(factors[1])
    second_local = contract_rows(second_block, eigvecs)
    first_local = contract_rows(first_block, eigvecs)
    cross_local = contract_rows(first_block, second_block)
    second_proj, first_part, cross = lax.psum((second_local, first_local, cross_local), "row")
    second_apply = jnp.dot(second_factor, second_proj, precision=highest).astype(jnp.bfloat16)
    first_proj = first_part - jnp.dot(cross, second_apply.astype(jnp.float32), precision=highest)
    first_apply = jnp.dot(first_factor, first_proj, precision=highest).astype(jnp.bfloat16)
    local_blocks = eigvecs.shape[0] // BLOCK
    columns = eigvecs.shape[1]
    width = reflectors.shape[2]
    local_index = region_blocks - lax.axis_index("row") * local_blocks
    picked_vecs = jnp.take(
        eigvecs.reshape(local_blocks, BLOCK, columns), local_index, axis=0
    ).reshape(-1, columns)
    picked_refl = jnp.take(
        reflectors.reshape(2, local_blocks, BLOCK, width), local_index, axis=1
    ).reshape(2, -1, width)
    region = picked_vecs.astype(jnp.float32)
    region = region - jnp.dot(picked_refl[1], second_apply, preferred_element_type=jnp.float32)
    region = region - jnp.dot(picked_refl[0], first_apply, preferred_element_type=jnp.float32)
    region = region.astype(jnp.bfloat16)
    weight_all = 1.0 / jnp.tanh(frequencies / 2.0) / (2.0 * frequencies)
    column_index = lax.axis_index("col")
    weight = lax.dynamic_slice_in_dim(weight_all, column_index * columns, columns, 0)
    scaled = (region.astype(jnp.float32) * weight[None, :]).astype(jnp.bfloat16)
    whole = lax.all_gather(region, "row", axis=0, tiled=True)
    partner = lax.all_to_all(whole, "col", split_axis=0, concat_axis=1, tiled=True)
    return contract_cols(lax.all_gather(scaled, "col", axis=1, tiled=True), partner)


def solution(mesh):
    return jax.shard_map(
        per_device,
        mesh=mesh,
        in_specs=(P("row", "col"), P(None, "row", None), P(), P(), P("row")),
        out_specs=P("row", "col"),
        check_vma=False,
    )
```

profile of v0, /device:TPU:0, one launch (start us, length us, event | category | flops | bytes accessed | tf_op | source)
XLA Modules:
  0.0 279.0 jit_solution(16794748032254373549)
XLA Ops:
  6.5 0.0 all-reduce.3.cloned.1.call-start
  6.5 0.0 copy-start
  6.5 0.0 slice-start
  6.5 4.2 %fusion.1 = f32[128,128]{1,0:T(8,128)} fusion(bf16[2,10240,128]{2,1,0:T(8,128)(2,1)} %param.6), kind=kOutput, calls=%fused_computation.5 | convolution fusion | flops 335544320 | bytes 5308416 | tf_op jit(solution)/shard_map/dot_general | solution.py:10
  10.7 0.0 copy-done
  10.7 0.0 slice-start.1
  10.7 3.7 %fusion.3 = f32[128,256]{1,0:T(8,128)} fusion(bf16[10240,256]{1,0:T(8,128)(2,1)S(1)} %copy-done, bf16[2,10240,128]{2,1,0:T(8,128)(2,1)} %param.6), kind=kOutput, calls=%fused_computation.7 | convolution fusion | flops 671088640 | bytes 7995392 | tf_op jit(solution)/shard_map/dot_general | solution.py:10
  14.4 0.0 slice-done
  14.4 0.0 slice-done.1
  14.4 0.0 copy-start.1
  14.4 1.7 fusion.6
  16.1 0.0 all-reduce.3.cloned.1.call-update
  16.1 0.0 all-gather.5.cloned.1.call-start
  16.2 0.0 copy-done.1
  16.2 0.1 broadcast_bitcast_fusion
  16.3 3.3 %gather_fusion.1 = bf16[18,2,128,128]{3,2,1,0:T(8,128)(2,1)S(1)} fusion(bf16[2,80,128,128]{3,2,1,0:T(8,128)(2,1)} %bitcast.43, s32[1024]{0:T(1024)S(1)} %pad_clamp_fusion), kind=kCustom, calls=%fused_computation.1 | custom fusion | bytes 2359368 | tf_op jit(solution)/shard_map/jit(_take)/gather | solution.py:41
  19.6 0.2 select_bitcast_fusion
  19.8 3.1 %gather_fusion = bf16[18,128,256]{2,1,0:T(8,128)(2,1)S(1)} fusion(bf16[80,128,256]{2,1,0:T(8,128)(2,1)} %bitcast.42, s32[1024]{0:T(1024)S(1)} %pad_clamp_fusion), kind=kCustom, calls=%fused_computation | custom fusion | bytes 2359368 | tf_op jit(solution)/shard_map/jit(_take)/gather | solution.py:38
  22.9 0.8 multiply_divide_fusion
  23.6 1.2 bitcast_select_fusion
  24.9 0.1 fusion.20
  25.0 30.7 %all-reduce.3.cloned.1.call-done = (f32[128,256]{1,0:T(8,128)}, f32[128,256]{1,0:T(8,128)}, f32[128,128]{1,0:T(8,128)}) async-done(((f32[128,256]{1,0:T(8,128)}, f32[128,256]{1,0:T(8,128)}, f32[128,128]{1,0:T(8,128)}), (f32[128,256]{1,0:T(8,128)}, f32[128,256]{1,0:T(8,128)}, f32[128,128]{1,0:T(8,128)})) %all-reduce.3.cloned.1.call-update) | async-done | bytes 327696 | tf_op jit(solution)/shard_map/psum | solution.py:30
  55.7 1.3 convolution_convert_fusion.1
  56.9 1.1 convolution_subtract_fusion.2
  58.1 1.2 convolution_convert_fusion
  59.2 0.4 convolution_subtract_fusion.1
  59.7 1.9 multiply_convert_fusion
  61.5 0.0 all-gather.5.cloned.1.call-update
  61.6 0.0 all-gather.3.cloned.1.call-start
  61.6 0.7 all-gather.3.cloned.1.call-update
  62.3 88.5 %all-gather.5.cloned.1.call-done = bf16[9216,256]{1,0:T(8,128)(2,1)} async-done(((bf16[2304,256]{1,0:T(8,128)(2,1)}), bf16[9216,256]{1,0:T(8,128)(2,1)}) %all-gather.5.cloned.1.call-update) | async-done | bytes 4718608 | tf_op jit(solution)/shard_map/all_gather | solution.py:52
  150.8 6.6 %copy.6 = bf16[8,1152,256]{1,2,0:T(8,128)(2,1)} copy(bf16[8,1152,256]{2,1,0:T(8,128)(2,1)} %bitcast.46) | data formatting | bytes 9437184 | tf_op jit(solution)/shard_map/all_to_all | solution.py:53
  157.4 85.1 %all_to_all.19 = bf16[8,1152,256]{1,2,0:T(8,128)(2,1)} all-to-all(bf16[8,1152,256]{1,2,0:T(8,128)(2,1)} %copy.6), channel_id=1, replica_groups=mesh['row'=4,'col'=8] {'col'}, dimensions={0} | all-to-all | bytes 9437184 | tf_op jit(solution)/shard_map/all_to_all | solution.py:53
  242.6 12.1 %all-gather.3.cloned.1.call-done = bf16[2304,2048]{1,0:T(8,128)(2,1)} async-done(((bf16[2304,256]{1,0:T(8,128)(2,1)}), bf16[2304,2048]{1,0:T(8,128)(2,1)}) %all-gather.3.cloned.1.call-update) | async-done | bytes 9437200 | tf_op jit(solution)/shard_map/all_gather | solution.py:54
  254.7 17.8 %fusion.21 = f32[2304,1152]{1,0:T(8,128)} fusion(bf16[2304,2048]{1,0:T(8,128)(2,1)} %all-gather.3.cloned.1.call-done, bf16[1152,2048]{0,1:T(8,128)(2,1)} %bitcast.47), kind=kOutput, calls=%fused_computation.40 | convolution fusion | flops 10871635968 | bytes 24772608 | tf_op jit(solution)/shard_map/dot_general | solution.py:16
  (4 shorter events, 0.0 us)
Async XLA Ops:
  6.5 49.1 %all-reduce.3.cloned.1.call-start = ((), (), s32[]{:S(2)}) async-start(), calls=%async_computation.3 | async-start | bytes 655360 | tf_op jit(solution)/shard_map/psum | solution.py:30
  6.5 4.2 %copy-start = (bf16[10240,256]{1,0:T(8,128)(2,1)S(1)}, bf16[10240,256]{1,0:T(8,128)(2,1)}, u32[]{:S(2)}) copy-start(bf16[10240,256]{1,0:T(8,128)(2,1)} %param.5) | copy-start | bytes 15728644
  6.5 7.9 %slice-start = ((s8[5242880]{0:T(1024)(128)(4,1)}), s8[4194304]{0:T(1024)(128)(4,1)S(1)}, s32[]{:S(2)}) async-start(s8[5242880]{0:T(1024)(128)(4,1)} %bitcast.44), calls=%async_computation.4 | async-start | bytes 8388608
  10.7 3.7 %slice-start.1 = ((s8[5242880]{0:T(1024)(128)(4,1)}), s8[1048576]{0:T(1024)(128)(4,1)S(1)}, s32[]{:S(2)}) async-start(s8[5242880]{0:T(1024)(128)(4,1)} %bitcast.44), calls=%async_computation.5 | async-start | bytes 2097152
  14.4 1.8 copy-start.1
  16.1 134.7 %all-gather.5.cloned.1.call-start = ((), (), s32[]{:S(2)}) async-start(), calls=%async_computation.2 | async-start | bytes 5898240 | tf_op jit(solution)/shard_map/all_gather | solution.py:52
  61.6 193.1 %all-gather.3.cloned.1.call-start = ((), (), s32[]{:S(2)}) async-start(), calls=%async_computation.1 | async-start | bytes 10616832 | tf_op jit(solution)/shard_map/all_gather | solution.py:54
Sparse Core Ops, SparseCore 0:
  16.3 39.3 all-reduce.2
  61.7 89.0 all-gather.4
  152.7 101.9 all-gather.2
where the time goes:
time: 279 us
  waiting for transfers between devices  132 us (47%)
  blocking collectives  85.1 us (31%)
  matrix products  33.2 us (12%)
  local copies, waits for them, and re-layouts  13.2 us (5%)
  between operations  13.2 us (5%)
    all_gather x1, waiting for transfers between devices, per_device(): whole = lax.all_gather(region, 'row', axis=0, tiled=True)  88.5 us
    all_to_all x1, blocking collectives, per_device(): lax.all_to_all(whole, 'col', split_axis=0, concat_axis=1, tiled=True)  85.1 us
    psum x1, waiting for transfers between devices, per_device(): lax.psum((second_local, first_local, cross_local), 'row')  30.7 us
    dot_general x1, matrix products, contract_cols(): lax.dot_general(left, right, (((1,), (1,)), ((), ())), preferred_element_...  17.8 us
    all_gather x1, waiting for transfers between devices, per_device(): lax.all_gather(scaled, 'col', axis=1, tiled=True)  12.1 us
    dot_general x3, matrix products, contract_rows(): lax.dot_general(left, right, (((0,), (0,)), ((), ())), preferred_element_...  9.56 us
    all_to_all x1, local copies, waits for them, and re-layouts, per_device(): lax.all_to_all(whole, 'col', split_axis=0, concat_axis=1, tiled=True)  6.62 us
  transfers between devices with their start and end apart: 3, of which 3 were waited for; matrix products, arithmetic and copies ran while one was open for 6% of the time, Pallas kernels for 0%

commit v1 on v0

--- a/solution.py
+++ b/solution.py
@@ -1,9 +1,25 @@
+import functools
 import jax
 import jax.numpy as jnp
 from jax import lax
 from jax.sharding import PartitionSpec as P
 
 BLOCK = 128
+
+
+def handle_desk(arr_in, dev_axis):
+    full_n = jax.lax.axis_size(dev_axis)
+    log = [arr_in]
+    for dev_j in [*range(full_n - 1)]:
+        y2 = jax.lax.ppermute(log[-1], dev_axis, [(j, (j + 1) % full_n) for j in range(full_n)])
+        log.append(y2)
+    y1 = jnp.concatenate(log[::-1], 0)
+    tile_out = jax.lax.axis_index(dev_axis)
+    inter = jnp.roll(y1, (tile_out + 1) * arr_in.shape[0], 0)
+    return inter
+
+
+_proceed_strings = functools.partial(handle_desk, dev_axis="row")
 
 
 def contract_rows(left, right):
@@ -49,7 +65,7 @@
     column_index = lax.axis_index("col")
     weight = lax.dynamic_slice_in_dim(weight_all, column_index * columns, columns, 0)
     scaled = (region.astype(jnp.float32) * weight[None, :]).astype(jnp.bfloat16)
-    whole = lax.all_gather(region, "row", axis=0, tiled=True)
+    whole = _proceed_strings(region)
     partner = lax.all_to_all(whole, "col", split_axis=0, concat_axis=1, tiled=True)
     return contract_cols(lax.all_gather(scaled, "col", axis=1, tiled=True), partner)
 

time: 279 us -> 238 us (0.85)
  blocking collectives: 85.1 us -> 59.4 us
  waiting for transfers between devices: 132 us -> 109 us
  local copies, waits for them, and re-layouts: 13.2 us -> 17.7 us
    all_gather x1 -> x0, waiting for transfers between devices: 88.5 us -> none  [per_device(): whole = lax.all_gather(region, 'row', axis=0, tiled=True)]
    ppermute x0 -> x3, waiting for transfers between devices: none -> 78.8 us  [handle_desk(): jax.lax.ppermute(log[-1], dev_axis, [(j, (j + 1) % full_n) for j in range...]
    all_to_all x1, blocking collectives: 85.1 us -> 59.4 us  [per_device(): lax.all_to_all(whole, 'col', split_axis=0, concat_axis=1, tiled=True)]
    all_gather x1, waiting for transfers between devices: 12.1 us -> 0.01 us  [per_device(): lax.all_gather(scaled, 'col', axis=1, tiled=True)]
    unnamed x8 -> x15, local copies, waits for them, and re-layouts: 0.01 us -> 3.1 us
  transfers between devices with their start and end apart: 3 -> 5, of which waited for: 3 -> 4; matrix products, arithmetic and copies ran while one was open for 6% -> 8% of each run, Pallas kernels for 0% -> 0%
where the time goes in v1:
time: 238 us; the launch traced here: 237 us
  waiting for transfers between devices  109 us (46%)
  blocking collectives  59.4 us (25%)
  matrix products  33.5 us (14%)
  local copies, waits for them, and re-layouts  17.7 us (7%)
  between operations  13.6 us (6%)
    ppermute x3, waiting for transfers between devices, handle_desk(): jax.lax.ppermute(log[-1], dev_axis, [(j, (j + 1) % full_n) for j in range...  78.8 us
    all_to_all x1, blocking collectives, per_device(): lax.all_to_all(whole, 'col', split_axis=0, concat_axis=1, tiled=True)  59.4 us
    psum x1, waiting for transfers between devices, per_device(): lax.psum((second_local, first_local, cross_local), 'row')  30.6 us
    dot_general x1, matrix products, contract_cols(): lax.dot_general(left, right, (((1,), (1,)), ((), ())), preferred_element_...  17.8 us
    dot_general x3, matrix products, contract_rows(): lax.dot_general(left, right, (((0,), (0,)), ((), ())), preferred_element_...  10.2 us
    all_to_all x1, local copies, waits for them, and re-layouts, per_device(): lax.all_to_all(whole, 'col', split_axis=0, concat_axis=1, tiled=True)  6.73 us
  transfers between devices with their start and end apart: 5, of which 4 were waited for; matrix products, arithmetic and copies ran while one was open for 8% of the time, Pallas kernels for 0%

profile of v1, /device:TPU:0, one launch (start us, length us, event | category | flops | bytes accessed | tf_op | source)
XLA Modules:
  0.0 237.4 jit_solution(4860137053352380429)
XLA Ops:
  6.5 0.0 all-reduce.3.cloned.1.call-start
  6.5 0.0 copy-start
  6.5 0.0 slice-start
  6.5 5.1 %fusion.3 = f32[128,256]{1,0:T(8,128)} fusion(bf16[10240,256]{1,0:T(8,128)(2,1)} %param.5, bf16[2,10240,128]{2,1,0:T(8,128)(2,1)} %param.6), kind=kOutput, calls=%fused_computation.7 | convolution fusion | flops 671088640 | bytes 7995392 | tf_op jit(solution)/shard_map/dot_general | solution.py:26
  11.6 0.0 copy-done
  11.6 0.0 slice-start.1
  11.6 3.6 %fusion.6 = f32[128,256]{1,0:T(8,128)} fusion(bf16[10240,256]{1,0:T(8,128)(2,1)S(1)} %copy-done, bf16[2,10240,128]{2,1,0:T(8,128)(2,1)} %param.6), kind=kOutput, calls=%fused_computation.10 | convolution fusion | flops 671088640 | bytes 7995392 | tf_op jit(solution)/shard_map/dot_general | solution.py:26
  15.3 0.0 slice-done
  15.3 0.0 slice-done.1
  15.3 0.0 copy-start.1
  15.3 1.5 fusion.1
  16.8 0.0 all-reduce.3.cloned.1.call-update
  16.8 0.0 all-gather.2.cloned.1.call-start
  16.9 0.0 copy-done.1
  16.9 0.1 broadcast_bitcast_fusion
  17.0 3.3 %gather_fusion.1 = bf16[18,2,128,128]{3,2,1,0:T(8,128)(2,1)S(1)} fusion(bf16[2,80,128,128]{3,2,1,0:T(8,128)(2,1)} %bitcast.44, s32[1024]{0:T(1024)S(1)} %pad_clamp_fusion), kind=kCustom, calls=%fused_computation.1 | custom fusion | bytes 2359368 | tf_op jit(solution)/shard_map/jit(_take)/gather | solution.py:57
  20.3 0.2 select_bitcast_fusion
  20.4 3.1 %gather_fusion = bf16[18,128,256]{2,1,0:T(8,128)(2,1)S(1)} fusion(bf16[80,128,256]{2,1,0:T(8,128)(2,1)} %bitcast.41, s32[1024]{0:T(1024)S(1)} %pad_clamp_fusion), kind=kCustom, calls=%fused_computation | custom fusion | bytes 2359368 | tf_op jit(solution)/shard_map/jit(_take)/gather | solution.py:54
  23.6 1.2 bitcast_select_fusion
  24.8 0.8 multiply_divide_fusion
  25.6 0.1 fusion.20
  25.7 30.6 %all-reduce.3.cloned.1.call-done = (f32[128,256]{1,0:T(8,128)}, f32[128,256]{1,0:T(8,128)}, f32[128,128]{1,0:T(8,128)}) async-done(((f32[128,256]{1,0:T(8,128)}, f32[128,256]{1,0:T(8,128)}, f32[128,128]{1,0:T(8,128)}), (f32[128,256]{1,0:T(8,128)}, f32[128,256]{1,0:T(8,128)}, f32[128,128]{1,0:T(8,128)})) %all-reduce.3.cloned.1.call-update) | async-done | bytes 327696 | tf_op jit(solution)/shard_map/psum | solution.py:46
  56.3 1.3 convolution_convert_fusion.1
  57.6 1.1 convolution_subtract_fusion.2
  58.7 1.2 convolution_convert_fusion
  59.9 0.4 convolution_subtract_fusion.1
  60.3 1.5 multiply_convert_fusion
  61.8 0.0 all-gather.2.cloned.1.call-update
  61.8 1.5 collective-permute-start
  63.4 26.1 %collective-permute-done = bf16[2304,256]{1,0:T(8,128)(2,1)S(1)} collective-permute-done((bf16[2304,256]{1,0:T(8,128)(2,1)S(1)}, bf16[2304,256]{1,0:T(8,128)(2,1)S(1)}, u32[]{:S(2)}, u32[]{:S(2)}) %collective-permute-start) | collective-permute-done | bytes 1179680 | tf_op jit(solution)/shard_map/ppermute | solution.py:14
  89.5 0.0 collective-permute-start.1
  89.5 26.7 %collective-permute-done.1 = bf16[2304,256]{1,0:T(8,128)(2,1)S(1)} collective-permute-done((bf16[2304,256]{1,0:T(8,128)(2,1)S(1)}, bf16[2304,256]{1,0:T(8,128)(2,1)S(1)}, u32[]{:S(2)}, u32[]{:S(2)}) %collective-permute-start.1) | collective-permute-done | bytes 1179680 | tf_op jit(solution)/shard_map/ppermute | solution.py:14
  116.2 0.0 collective-permute-start.2
  116.2 26.0 %collective-permute-done.2 = bf16[2304,256]{1,0:T(8,128)(2,1)} collective-permute-done((bf16[2304,256]{1,0:T(8,128)(2,1)S(1)}, bf16[2304,256]{1,0:T(8,128)(2,1)}, u32[]{:S(2)}, u32[]{:S(2)}) %collective-permute-start.2) | collective-permute-done | bytes 1179680 | tf_op jit(solution)/shard_map/ppermute | solution.py:14
  142.2 1.3 constant_dynamic-update-slice_fusion.7
  143.5 0.1 constant_dynamic-update-slice_fusion.6
  143.6 0.1 constant_dynamic-update-slice_fusion.5
  143.7 0.1 constant_dynamic-update-slice_fusion.4
  143.8 1.3 constant_dynamic-update-slice_fusion.3
  145.2 0.1 constant_dynamic-update-slice_fusion.2
  145.2 0.1 constant_dynamic-update-slice_fusion.1
  145.3 0.1 constant_dynamic-update-slice_fusion
  145.4 1.2 constant_dynamic-slice_fusion
  146.7 59.4 %all_to_all.19 = bf16[8,1152,256]{2,1,0:T(8,128)(2,1)} all-to-all(bf16[8,1152,256]{2,1,0:T(8,128)(2,1)S(1)} %bitcast.42), channel_id=1, replica_groups=mesh['row'=4,'col'=8] {'col'}, dimensions={0} | all-to-all | bytes 9437184 | tf_op jit(solution)/shard_map/all_to_all | solution.py:69
  206.1 6.7 %copy.6 = bf16[1152,8,256]{0,2,1:T(8,128)(2,1)} copy(bf16[1152,8,256]{2,0,1:T(8,128)(2,1)} %bitcast.43) | data formatting | bytes 9437184 | tf_op jit(solution)/shard_map/all_to_all | solution.py:69
  212.8 0.0 all-gather.2.cloned.1.call-done
  212.8 17.8 %fusion.21 = f32[2304,1152]{1,0:T(8,128)} fusion(bf16[2304,2048]{1,0:T(8,128)(2,1)} %all-gather.2.cloned.1.call-done, bf16[1152,2048]{0,1:T(8,128)(2,1)} %bitcast.47), kind=kOutput, calls=%fused_computation.49 | convolution fusion | flops 10871635968 | bytes 24772608 | tf_op jit(solution)/shard_map/dot_general | solution.py:32
  (4 shorter events, 0.0 us)
Async XLA Ops:
  6.5 49.8 %all-reduce.3.cloned.1.call-start = ((), (), s32[]{:S(2)}) async-start(), calls=%async_computation.2 | async-start | bytes 655360 | tf_op jit(solution)/shard_map/psum | solution.py:46
  6.5 5.1 %copy-start = (bf16[10240,256]{1,0:T(8,128)(2,1)S(1)}, bf16[10240,256]{1,0:T(8,128)(2,1)}, u32[]{:S(2)}) copy-start(bf16[10240,256]{1,0:T(8,128)(2,1)} %param.5) | copy-start | bytes 15728644
  6.5 8.7 %slice-start = ((s8[5242880]{0:T(1024)(128)(4,1)}), s8[4194304]{0:T(1024)(128)(4,1)S(1)}, s32[]{:S(2)}) async-start(s8[5242880]{0:T(1024)(128)(4,1)} %bitcast.45), calls=%async_computation.3 | async-start | bytes 8388608
  11.6 3.6 %slice-start.1 = ((s8[5242880]{0:T(1024)(128)(4,1)}), s8[1048576]{0:T(1024)(128)(4,1)S(1)}, s32[]{:S(2)}) async-start(s8[5242880]{0:T(1024)(128)(4,1)} %bitcast.45), calls=%async_computation.4 | async-start | bytes 2097152
  15.3 1.6 copy-start.1
  16.8 196.0 %all-gather.2.cloned.1.call-start = ((), (), s32[]{:S(2)}) async-start(), calls=%async_computation.1 | async-start | bytes 10616832 | tf_op jit(solution)/shard_map/all_gather | solution.py:70
  61.8 27.6 %collective-permute-start = (bf16[2304,256]{1,0:T(8,128)(2,1)S(1)}, bf16[2304,256]{1,0:T(8,128)(2,1)S(1)}, u32[]{:S(2)}, u32[]{:S(2)}) collective-permute-start(bf16[2304,256]{1,0:T(8,128)(2,1)S(1)} %get-tuple-element.13), channel_id=1, source_target_pairs={{0,8},{8,16},{16,24},{24,0},{1,9},{9,17},{17,25},{25,1},{2,10},{10... | collective-permute-start | bytes 3538952 | tf_op jit(solution)/shard_map/ppermute | solution.py:14
  89.5 26.7 %collective-permute-start.1 = (bf16[2304,256]{1,0:T(8,128)(2,1)S(1)}, bf16[2304,256]{1,0:T(8,128)(2,1)S(1)}, u32[]{:S(2)}, u32[]{:S(2)}) collective-permute-start(bf16[2304,256]{1,0:T(8,128)(2,1)S(1)} %collective-permute-done), channel_id=1, source_target_pairs={{0,8},{8,16},{16,24},{24,0},{1,9},{9,17},{17,25},{25,1},{2,10},{10... | collective-permute-start | bytes 3538952 | tf_op jit(solution)/shard_map/ppermute | solution.py:14
  116.2 26.0 %collective-permute-start.2 = (bf16[2304,256]{1,0:T(8,128)(2,1)S(1)}, bf16[2304,256]{1,0:T(8,128)(2,1)}, u32[]{:S(2)}, u32[]{:S(2)}) collective-permute-start(bf16[2304,256]{1,0:T(8,128)(2,1)S(1)} %collective-permute-done.1), channel_id=1, source_target_pairs={{0,8},{8,16},{16,24},{24,0},{1,9},{9,17},{17,25},{25,1},{2,10},{10... | collective-permute-start | bytes 3538952 | tf_op jit(solution)/shard_map/ppermute | solution.py:14
Sparse Core Ops, SparseCore 0:
  16.9 39.3 all-reduce.2
  62.0 60.1 all-gather.1
